TPU v7x, 32 devices: a whole 2x2x4 slice. The times are simulated.
32 devices in a mesh: seg: 4 (over y, x), lat: 8 (over z, core).
Axes of the slice: x: 2, y: 2, z: 4, core: 2. Of those that a mesh axis runs over, the one named last changes fastest.
Arguments:
- coh_map: bfloat16 [4, 65536, 128], P('seg', 'lat'), may hold values from 0 to 40, as said below
- positions: int32 [4, 1024], P('seg', 'lat'), may hold values from 0 to 16776959, as said below
- counts: int32 [16], P('lat'), may hold values from 1 to 64, as said below
Outputs:
- semi_stat: bfloat16 [1024, 128], P('lat')
- excess: float32 [16, 128], P('lat')
Inputs may be any that keep to these rules, and one draw needn't show every extreme that they name: `coh_map`: nonnegative. `counts`: the first block has 1 valid point and the last block 64. `positions`: the bins are split into 8 aligned slices of 8192 bins; a point's two bins lie in the same slice; in each segment, at most 32 of the 128 points of one index of lat have their bins in one slice, and that most is reached in every draw.
All inputs are finite; a program needn't handle non-finite values.
Results may differ from a plain program's by a relative error of at most 0.001.
Values sent between devices are 32-bit elements; how exact they have to be, the bound alone decides.
A program may use at most 64 MiB of HBM per device.

v0:
```python
import jax
import jax.numpy as jnp
from jax import lax
from jax.sharding import PartitionSpec as P


def routed_sums(positions, coh_map, first_bin):
    seg_count = coh_map.shape[0]
    slice_bins = coh_map.shape[1]
    width = coh_map.shape[2]
    own_rows = positions.shape[1]
    n_lataxis = lax.axis_size("lat")
    slot_limit = 2 * own_rows // n_lataxis
    dest = positions // 256 // slice_bins
    dest_hits = (dest[:, :, None] == lax.broadcasted_iota(jnp.int32, (1, 1, n_lataxis), 2)).astype(
        jnp.int32
    )
    before = jnp.cumsum(dest_hits, axis=1) - dest_hits
    slot = jnp.sum(before * dest_hits, axis=2)
    seg_ids = lax.broadcasted_iota(jnp.int32, positions.shape, 0)
    outgoing = (
        jnp.full((n_lataxis, seg_count, slot_limit), -1, jnp.int32)
        .at[dest, seg_ids, slot]
        .set(positions)
    )
    bin_index = lax.broadcasted_iota(jnp.int32, (1, slice_bins), 1)
    incoming = lax.all_to_all(outgoing, "lat", split_axis=0, concat_axis=0, tiled=True)
    item_count = incoming.shape[2]
    pos_flat = incoming[:, 0, :].reshape(-1)
    live = (pos_flat >= 0)[:, None]
    rel_bin = (pos_flat // 256 - first_bin)[:, None]
    fraction = (pos_flat % 256).astype(jnp.float32)[:, None] / 256.0
    weights = jnp.where(live & (bin_index == rel_bin), 1.0 - fraction, 0.0) + jnp.where(
        live & (bin_index == rel_bin + 1), fraction, 0.0
    )
    rows = jnp.dot(weights.astype(jnp.bfloat16), coh_map[0], preferred_element_type=jnp.float32)
    row_list = [rows.reshape(n_lataxis, item_count, width)]
    stacked = jnp.stack(row_list, axis=1)
    returned = lax.all_to_all(stacked, "lat", split_axis=0, concat_axis=0, tiled=True)
    by_segment = returned.transpose(1, 0, 2, 3).reshape(seg_count, n_lataxis * slot_limit, width)
    flat_index = dest * slot_limit + slot
    picked = jnp.take_along_axis(by_segment, flat_index[:, :, None], axis=1)
    return jnp.sum(picked, axis=0)


def shards(coh_map, positions, counts):
    seg_count = coh_map.shape[0]
    slice_bins = coh_map.shape[1]
    first_bin = lax.axis_index("lat") * slice_bins
    n_segaxis = lax.axis_size("seg")
    total_segs = seg_count * n_segaxis
    own_rows = positions.shape[1]
    local_sums_rows = routed_sums(positions, coh_map, first_bin)
    summed = lax.psum(local_sums_rows, "seg")
    semi_stat = summed / total_segs
    block_count = counts.shape[0]
    block_size = own_rows // block_count
    grouped = semi_stat.reshape(block_count, block_size, semi_stat.shape[1])
    slot_index = lax.broadcasted_iota(jnp.int32, (block_count, block_size, 1), 1)
    live_mask = slot_index < counts[:, None, None]
    block_sums = jnp.sum(jnp.where(live_mask, grouped, 0.0), axis=1)
    count_float = counts.astype(jnp.float32)
    block_means = block_sums / count_float[:, None]
    column_sums, total_count = lax.psum((jnp.sum(block_sums, axis=0), jnp.sum(count_float)), "lat")
    global_mean = column_sums / total_count
    excess = block_means - global_mean[None, :]
    return (semi_stat.astype(jnp.bfloat16), excess)


def solution(mesh):
    in_specs = (P("seg", "lat", None), P("seg", "lat"), P("lat"))
    out_specs = (P("lat", None), P("lat", None))
    return jax.shard_map(shards, mesh=mesh, in_specs=in_specs, out_specs=out_specs, check_vma=False)
```

profile of v0, /device:TPU:0, one launch (start us, length us, event | category | flops | bytes accessed | tf_op | source)
XLA Modules:
  0.0 125.4 jit_solution(7126655053401794815)
XLA Ops:
  7.2 0.0 copy-start
  7.2 0.8 fusion.19
  8.0 0.1 fusion.12
  8.1 0.2 reduce_window_sum.11
  8.3 0.2 select_reduce_fusion.2
  8.5 0.6 broadcast.427
  9.1 19.9 %scatter_fusion = s32[8,32]{1,0:T(8,128)} fusion(s32[8,32]{1,0:T(8,128)} %broadcast.427, s32[128]{0:T(128)S(1)} %fusion.21, s32[128]{0:T(128)} %bitcast.50), kind=kCustom, calls=%fused_computation.1 | custom fusion | bytes 2560 | tf_op jit(solution)/shard_map/scatter | solution.py:24
  29.0 6.4 %all-to-all-start = ((s32[8,1,32]{2,1,0:T(1,128)}), s32[8,1,32]{2,1,0:T(1,128)S(1)}, u32[]{:S(2)}, u32[]{:S(2)}) async-start(s32[8,1,32]{2,1,0:T(1,128)} %bitcast.9), calls=%async_computation | async-start | bytes 8192 | tf_op jit(solution)/shard_map/all_to_all | solution.py:27
  35.3 0.7 iota_compare_fusion.3
  36.0 4.8 %all-to-all-done = s32[8,1,32]{2,1,0:T(1,128)S(1)} async-done(((s32[8,1,32]{2,1,0:T(1,128)}), s32[8,1,32]{2,1,0:T(1,128)S(1)}, u32[]{:S(2)}, u32[]{:S(2)}) %all-to-all-start) | async-done | bytes 1056 | tf_op jit(solution)/shard_map/all_to_all | solution.py:27
  40.9 0.0 copy-done
  40.9 0.0 copy-start.1
  40.9 5.0 %fusion.7 = f32[8,1,32,128]{3,2,1,0:T(8,128)} fusion(bf16[1,8192,128]{2,1,0:T(8,128)(2,1)S(1)} %copy-done, f32[8,32]{1,0:T(8,128)S(1)} %get-tuple-element.5, s32[8,32]{1,0:T(8,128)S(1)} %get-tuple-element.6, f32[8,32]{1,0:T(8,128)S(1)} %get-tuple-element.4, s32[8,32]{1,0:T(8,128)S(1)} %get-tuple-element.7, pred[8,32]{1,0:T(8,128)(4,1)S(1)} %broadcast_compare_fusion), kind=kOutput, calls=%fused_computation.11 | convolution fusion | flops 553648128 | bytes 2232576 | tf_op jit(solution)/shard_map/dot_general | solution.py:36
  45.9 3.4 %all-to-all-start.1 = ((f32[8,1,32,128]{3,2,1,0:T(8,128)}), f32[8,1,32,128]{3,2,1,0:T(8,128)S(1)}, u32[]{:S(2)}, u32[]{:S(2)}) async-start(f32[8,1,32,128]{3,2,1,0:T(8,128)} %fusion.7), calls=%async_computation.1 | async-start | bytes 262144 | tf_op jit(solution)/shard_map/all_to_all | solution.py:39
  49.2 0.0 all-reduce.3.cloned.1.call-start
  49.3 0.0 copy-done.1
  49.3 0.1 lt.77
  49.4 6.5 %all-to-all-done.1 = f32[8,1,32,128]{3,2,1,0:T(8,128)S(1)} async-done(((f32[8,1,32,128]{3,2,1,0:T(8,128)}), f32[8,1,32,128]{3,2,1,0:T(8,128)S(1)}, u32[]{:S(2)}, u32[]{:S(2)}) %all-to-all-start.1) | async-done | bytes 131104 | tf_op jit(solution)/shard_map/all_to_all | solution.py:39
  55.9 0.6 gather_fusion
  56.6 0.7 broadcast_select_fusion
  57.3 0.0 all-reduce.3.cloned.1.call-update
  57.3 0.6 convert_reduce_fusion
  57.9 40.4 %all-reduce.3.cloned.1.call-done = f32[128,128]{1,0:T(8,128)} async-done(((f32[128,128]{1,0:T(8,128)}), f32[128,128]{1,0:T(8,128)}) %all-reduce.3.cloned.1.call-update) | async-done | bytes 65552 | tf_op jit(solution)/shard_map/psum | solution.py:54
  98.3 1.5 %select_reduce_fusion = (f32[128]{0:T(128)S(1)}, bf16[128,128]{1,0:T(8,128)(2,1)}) fusion(pred[128]{0:T(512)(128)(4,1)S(1)} %lt.77, f32[128,128]{1,0:T(8,128)} %all-reduce.3.cloned.1.call-done), kind=kLoop, calls=%fused_computation.12 | loop fusion | flops 65408 | bytes 98944 | tf_op jit(solution)/shard_map/reduce_sum | solution.py:64
  99.8 16.6 %all-reduce = (f32[128]{0:T(128)S(1)}, f32[]{:T(128)}) all-reduce(f32[128]{0:T(128)S(1)} %get-tuple-element.10, f32[]{:T(128)} %convert_reduce_fusion), channel_id=1, replica_groups=mesh['seg'=4,'lat'=8] {'lat'}, use_global_device_ids=true, to_apply=%region_6.7 | all-reduce | flops 129 | bytes 1032 | tf_op jit(solution)/shard_map/psum | solution.py:64
  116.3 0.6 broadcast_divide_fusion
  117.0 0.9 select_reduce_fusion.1
  117.9 0.6 divide_subtract_fusion
  (11 shorter events, 0.1 us)
Async XLA Ops:
  7.2 33.7 %copy-start = (bf16[1,8192,128]{2,1,0:T(8,128)(2,1)S(1)}, bf16[1,8192,128]{2,1,0:T(8,128)(2,1)}, u32[]{:S(2)}) copy-start(bf16[1,8192,128]{2,1,0:T(8,128)(2,1)} %param.3) | copy-start | bytes 6291460
  29.0 11.9 %all-to-all-start = ((s32[8,1,32]{2,1,0:T(1,128)}), s32[8,1,32]{2,1,0:T(1,128)S(1)}, u32[]{:S(2)}, u32[]{:S(2)}) async-start(s32[8,1,32]{2,1,0:T(1,128)} %bitcast.9), calls=%async_computation | async-start | bytes 8192 | tf_op jit(solution)/shard_map/all_to_all | solution.py:27
  40.9 8.4 %copy-start.1 = (s32[2]{0:T(128)S(1)}, s32[2]{0:T(128)}, u32[]{:S(2)}) copy-start(s32[2]{0:T(128)} %param.5) | copy-start | bytes 28
  45.9 10.1 %all-to-all-start.1 = ((f32[8,1,32,128]{3,2,1,0:T(8,128)}), f32[8,1,32,128]{3,2,1,0:T(8,128)S(1)}, u32[]{:S(2)}, u32[]{:S(2)}) async-start(f32[8,1,32,128]{3,2,1,0:T(8,128)} %fusion.7), calls=%async_computation.1 | async-start | bytes 262144 | tf_op jit(solution)/shard_map/all_to_all | solution.py:39
  49.2 49.1 %all-reduce.3.cloned.1.call-start = ((), (), s32[]{:S(2)}) async-start(), calls=%async_computation.2 | async-start | bytes 131072 | tf_op jit(solution)/shard_map/psum | solution.py:54
Sparse Core Ops, SparseCore 0:
  57.4 40.8 all-reduce.2
where the time goes:
time: 126 us; the launch traced here: 125 us
  waiting for transfers between devices  51.7 us (41%)
  local copies, waits for them, and re-layouts  21.2 us (17%)
  blocking collectives  16.6 us (13%)
  between operations  14.1 us (11%)
  starting transfers between devices  9.76 us (8%)
  other arithmetic  7.05 us (6%)
  matrix products  4.96 us (4%)
    psum x1, waiting for transfers between devices, shards(): summed = lax.psum(local_sums_rows, 'seg')  40.4 us
    scatter x1, local copies, waits for them, and re-layouts, routed_sums(): outgoing = jnp.full((n_lataxis, seg_count, slot_limit), -1, jnp.int32).at...  19.9 us
    psum x1, blocking collectives, shards(): lax.psum((jnp.sum(block_sums, axis=0), jnp.sum(count_float)), 'lat')  16.6 us
    all_to_all x1, waiting for transfers between devices, routed_sums(): lax.all_to_all(stacked, 'lat', split_axis=0, concat_axis=0, tiled=True)  6.51 us
    all_to_all x1, starting transfers between devices, routed_sums(): lax.all_to_all(outgoing, 'lat', split_axis=0, concat_axis=0, tiled=True)  6.35 us
    dot_general x1, matrix products, routed_sums(): jnp.dot(weights.astype(jnp.bfloat16), coh_map[0], preferred_element_type=...  4.96 us
    all_to_all x1, waiting for transfers between devices, routed_sums(): lax.all_to_all(outgoing, 'lat', split_axis=0, concat_axis=0, tiled=True)  4.77 us
    all_to_all x1, starting transfers between devices, routed_sums(): lax.all_to_all(stacked, 'lat', split_axis=0, concat_axis=0, tiled=True)  3.37 us
  transfers between devices with their start and end apart: 3, of which 3 were waited for; matrix products, arithmetic and copies ran while one was open for 1% of the time, Pallas kernels for 0%

commit v1 on v0

v1 whole, which is shorter than its diff:
```python
import functools

import jax
import jax.numpy as jnp
from jax import lax
from jax.experimental import pallas as pl
from jax.experimental.pallas import tpu as pltpu
from jax.sharding import PartitionSpec as P

MESH = pl.DeviceIdType.MESH
PIECES = 4


def kernel(
    n_lat,
    n_seg,
    pos_ref,
    cnt_ref,
    coh_hbm,
    semi_ref,
    excess_ref,
    coh,
    gath,
    rows_out,
    rows_in,
    col_out,
    col_in,
    part,
    part_in,
    psum,
    psum_in,
    coh_sem,
    gs_sem,
    gr_sem,
    rs_sem,
    rr_sem,
    cs_sem,
    cr_sem,
    xs_sem,
    xr_sem,
):
    lat = lax.axis_index("lat")
    seg = lax.axis_index("seg")
    slice_bins, width = coh.shape
    points = pos_ref.shape[1]
    blocks = cnt_ref.shape[0]
    block_size = points // blocks
    slots = 2 * points // n_lat
    total_slots = n_lat * slots
    steps = n_seg.bit_length() - 1
    f32, bf16, i32 = jnp.float32, jnp.bfloat16, jnp.int32

    piece = slice_bins // PIECES
    loads = []
    for k in range(PIECES):
        rng = pl.ds(k * piece, piece)
        loads.append(pltpu.make_async_copy(coh_hbm.at[0, rng], coh.at[rng], coh_sem.at[k]))
        loads[-1].start()

    barrier = pltpu.get_barrier_semaphore()
    lat_peers = [lax.rem(lat + j, n_lat) for j in range(n_lat)]
    lat_back = [lax.rem(lat + n_lat - j, n_lat) for j in range(n_lat)]
    seg_peers = []
    for b in range(steps):
        w = 1 << b
        bit = lax.rem(seg // w, 2)
        seg_peers.append(seg + w - 2 * w * bit)
    for j in range(1, n_lat):
        pl.semaphore_signal(barrier, inc=1, device_id=(seg, lat_peers[j]), device_id_type=MESH)
    for b in range(steps):
        pl.semaphore_signal(barrier, inc=1, device_id=(seg_peers[b], lat), device_id_type=MESH)

    pos = pos_ref[...]
    lane = lax.broadcasted_iota(i32, (1, points), 1)
    dest = (pos // 256) // slice_bins
    rel = lax.rem(dest - lat + n_lat, n_lat)
    hits = lax.broadcasted_iota(i32, (n_lat, points), 0) == rel
    hits_f = hits.astype(f32)
    tri = (
        lax.broadcasted_iota(i32, (points, points), 0)
        < lax.broadcasted_iota(i32, (points, points), 1)
    ).astype(f32)
    before = jnp.dot(hits_f.astype(bf16), tri.astype(bf16), preferred_element_type=f32)
    slot = jnp.sum(before * hits_f, axis=0, keepdims=True).astype(i32)
    sid = rel * slots + slot
    limit = jnp.zeros((1, points), i32)
    for b in range(blocks):
        limit = jnp.where(lane // block_size == b, cnt_ref[b], limit)
    valid = (lane % block_size < limit).astype(i32)
    gath[0, 0:1, :] = sid
    gath[0, 1:2, :] = pos
    gath[0, 2:3, :] = valid
    gath[0, 3:4, :] = valid

    pl.semaphore_wait(barrier, n_lat - 1 + steps)
    sends = []
    for j in range(1, n_lat):
        copy = pltpu.make_async_remote_copy(
            src_ref=gath.at[0],
            dst_ref=gath.at[j],
            send_sem=gs_sem.at[j],
            recv_sem=gr_sem.at[j],
            device_id=(seg, lat_peers[j]),
            device_id_type=MESH,
        )
        copy.start()
        sends.append(copy)

    pick_t = (lax.broadcasted_iota(i32, (total_slots, points), 0) == sid).astype(f32)
    pick = pick_t.T.astype(bf16)

    for copy in sends:
        copy.wait_recv()

    base = lat * (slice_bins * 256)
    flag = slice_bins * 256
    sub = lax.broadcasted_iota(i32, (slots, points), 0)
    cols = []
    count = jnp.zeros((1, points), i32)
    for j in range(n_lat):
        code = (gath[j, 1:2, :] - base + flag * (1 + gath[j, 2:3, :])).astype(f32)
        here = (gath[j, 0:1, :] - j * slots) == sub
        cols.append(jnp.sum(jnp.where(here, code, 0.0), axis=1, keepdims=True))
        count = count + gath[j, 2:3, :]
    code = jnp.concatenate(cols, axis=0).astype(i32)
    total_count = jnp.sum(count.astype(f32), axis=1, keepdims=True)
    present = code >= flag
    live = code >= 2 * flag
    off = code % flag
    low = off // 256
    upper = (off % 256).astype(f32) / 256.0
    depth = min(256, slice_bins)
    chunk = low // depth
    in_chunk = low % depth
    bins = lax.broadcasted_iota(i32, (total_slots, depth), 1)
    local = jnp.where(bins == in_chunk, 1.0 - upper, 0.0) + jnp.where(
        bins == (in_chunk + 1) % depth, upper, 0.0
    )
    where_id = jnp.where(bins < in_chunk, chunk + 1, chunk)
    where_id = jnp.where(present, where_id, -1)
    local = local.astype(bf16)
    where_id = where_id.astype(f32).astype(bf16)
    zero = jnp.zeros_like(local)

    held = jnp.zeros((total_slots, width), f32)
    per_piece = piece // depth
    for k in range(PIECES):
        loads[k].wait()
        weights = jnp.concatenate(
            [
                jnp.where(where_id == jnp.asarray(k * per_piece + c, bf16), local, zero)
                for c in range(per_piece)
            ],
            axis=1,
        )
        held = held + jnp.dot(
            weights, coh[k * piece : (k + 1) * piece, :], preferred_element_type=f32
        )

    col = jnp.sum(jnp.where(live, held, 0.0), axis=0, keepdims=True)
    for j in range(n_lat):
        rows_out[j] = held[j * slots : (j + 1) * slots, :]
    col_out[...] = col
    back = []
    for j in range(1, n_lat):
        copy = pltpu.make_async_remote_copy(
            src_ref=rows_out.at[j],
            dst_ref=rows_in.at[j],
            send_sem=rs_sem.at[j],
            recv_sem=rr_sem.at[j],
            device_id=(seg, lat_back[j]),
            device_id_type=MESH,
        )
        copy.start()
        back.append(copy)
        copy = pltpu.make_async_remote_copy(
            src_ref=col_out,
            dst_ref=col_in.at[j],
            send_sem=cs_sem.at[j],
            recv_sem=cr_sem.at[j],
            device_id=(seg, lat_back[j]),
            device_id_type=MESH,
        )
        copy.start()
        back.append(copy)
    for copy in back:
        copy.wait_recv()

    own = [rows_out[0]] + [rows_in[j] for j in range(1, n_lat)]
    got = jnp.concatenate(own, axis=0)
    high = got.astype(bf16)
    rest = (got - high.astype(f32)).astype(bf16)
    total = jnp.dot(pick, high, preferred_element_type=f32) + jnp.dot(
        pick, rest, preferred_element_type=f32
    )
    for j in range(1, n_lat):
        col = col + col_in[j]

    half = points // 2
    halves = [total[:half], total[half:]]
    outs = []
    for t in range(steps):
        moves = []
        order = (t, steps - 1 - t)
        for h in range(2):
            part[t, h] = halves[h]
        psum[t] = col
        for h in range(2):
            copy = pltpu.make_async_remote_copy(
                src_ref=part.at[t, h],
                dst_ref=part_in.at[t, h],
                send_sem=xs_sem.at[t, h],
                recv_sem=xr_sem.at[t, h],
                device_id=(seg_peers[order[h]], lat),
                device_id_type=MESH,
            )
            copy.start()
            moves.append(copy)
        copy = pltpu.make_async_remote_copy(
            src_ref=psum.at[t],
            dst_ref=psum_in.at[t],
            send_sem=xs_sem.at[t, 2],
            recv_sem=xr_sem.at[t, 2],
            device_id=(seg_peers[order[0]], lat),
            device_id_type=MESH,
        )
        copy.start()
        moves.append(copy)
        for copy in moves:
            copy.wait_recv()
        halves = [halves[h] + part_in[t, h] for h in range(2)]
        col = col + psum_in[t]
        outs += moves

    stat = jnp.concatenate(halves, axis=0) / n_seg
    semi_ref[...] = stat.astype(semi_ref.dtype)
    global_mean = (col / n_seg) / total_count
    row = lax.broadcasted_iota(i32, (block_size, width), 0)
    for b in range(blocks):
        block = stat[b * block_size : (b + 1) * block_size]
        block_sum = jnp.sum(jnp.where(row < cnt_ref[b], block, 0.0), axis=0, keepdims=True)
        mean = block_sum / jnp.full((1, width), cnt_ref[b], i32).astype(f32)
        excess_ref[b : b + 1, :] = mean - global_mean

    for copy in sends + back + outs:
        copy.wait_send()


def shards(n_lat, n_seg, coh_map, positions, counts):
    _, slice_bins, width = coh_map.shape
    points = positions.shape[1]
    blocks = counts.shape[0]
    slots = 2 * points // n_lat
    steps = n_seg.bit_length() - 1
    f32 = jnp.float32
    dma = pltpu.SemaphoreType.DMA
    return pl.pallas_call(
        functools.partial(kernel, n_lat, n_seg),
        out_shape=(
            jax.ShapeDtypeStruct((points, width), jnp.bfloat16),
            jax.ShapeDtypeStruct((blocks, width), f32),
        ),
        in_specs=[
            pl.BlockSpec(memory_space=pltpu.VMEM),
            pl.BlockSpec(memory_space=pltpu.SMEM),
            pl.BlockSpec(memory_space=pl.ANY),
        ],
        out_specs=(
            pl.BlockSpec(memory_space=pltpu.VMEM),
            pl.BlockSpec(memory_space=pltpu.VMEM),
        ),
        scratch_shapes=[
            pltpu.VMEM((slice_bins, width), coh_map.dtype),
            pltpu.VMEM((n_lat, 4, points), jnp.int32),
            pltpu.VMEM((n_lat, slots, width), f32),
            pltpu.VMEM((n_lat, slots, width), f32),
            pltpu.VMEM((1, width), f32),
            pltpu.VMEM((n_lat, 1, width), f32),
            pltpu.VMEM((steps, 2, points // 2, width), f32),
            pltpu.VMEM((steps, 2, points // 2, width), f32),
            pltpu.VMEM((steps, 1, width), f32),
            pltpu.VMEM((steps, 1, width), f32),
            dma((PIECES,)),
            dma((n_lat,)),
            dma((n_lat,)),
            dma((n_lat,)),
            dma((n_lat,)),
            dma((n_lat,)),
            dma((n_lat,)),
            dma((steps, 3)),
            dma((steps, 3)),
        ],
        compiler_params=pltpu.CompilerParams(collective_id=0, has_side_effects=True),
    )(positions, counts, coh_map)


def solution(mesh):
    in_specs = (P("seg", "lat", None), P("seg", "lat"), P("lat"))
    out_specs = (P("lat", None), P("lat", None))
    body = functools.partial(shards, mesh.shape["lat"], mesh.shape["seg"])
    return jax.shard_map(body, mesh=mesh, in_specs=in_specs, out_specs=out_specs, check_vma=False)
```

time: 126 us -> 28.9 us (0.23)
  waiting for transfers between devices: 51.7 us -> 0 us
  Pallas kernels: 0 us -> 25.4 us
  local copies, waits for them, and re-layouts: 21.2 us -> 2.6 us
  blocking collectives: 16.6 us -> 0 us
  between operations: 14.1 us -> 0.64 us
  starting transfers between devices: 9.76 us -> 0 us
  other arithmetic: 7.05 us -> 0 us
  matrix products: 4.96 us -> 0 us
    psum x1 -> x0, waiting for transfers between devices: 40.4 us -> none  [shards(): summed = lax.psum(local_sums_rows, 'seg')]
    pallas_call x0 -> x1, Pallas kernels: none -> 25.4 us  [shards(): pl.pallas_call(functools.partial(kernel, n_lat, n_seg), out_shape=(jax.Sh...]
    scatter x1 -> x0, local copies, waits for them, and re-layouts: 19.9 us -> none  [routed_sums(): outgoing = jnp.full((n_lataxis, seg_count, slot_limit), -1, jnp.int32).at...]
    psum x1 -> x0, blocking collectives: 16.6 us -> none  [shards(): lax.psum((jnp.sum(block_sums, axis=0), jnp.sum(count_float)), 'lat')]
    all_to_all x2 -> x0, waiting for transfers between devices: 11.3 us -> none  [the longest x1 6.51 us: routed_sums(): lax.all_to_all(stacked, 'lat', split_axis=0, concat_axis=0, tiled=True)]
    all_to_all x2 -> x0, starting transfers between devices: 9.72 us -> none  [the longest x1 6.35 us: routed_sums(): lax.all_to_all(outgoing, 'lat', split_axis=0, concat_axis=0, tiled=True)]
    dot_general x1 -> x0, matrix products: 4.96 us -> none  [routed_sums(): jnp.dot(weights.astype(jnp.bfloat16), coh_map[0], preferred_element_type=...]
    reduce_sum x4 -> x0, other arithmetic: 3.17 us -> none  [the longest x1 1.46 us: shards(): jnp.sum(block_sums, axis=0)]
  transfers between devices with their start and end apart: 3 -> 0, of which waited for: 3 -> 0; matrix products, arithmetic and copies ran while one was open for 1% -> 0% of each run, Pallas kernels for 0% -> 0%
where the time goes in v1:
time: 28.9 us; the launch traced here: 28.7 us
  Pallas kernels  25.4 us (88%)
  local copies, waits for them, and re-layouts  2.6 us (9%)
  between operations  0.64 us (2%)
    pallas_call x1, Pallas kernels, shards(): pl.pallas_call(functools.partial(kernel, n_lat, n_seg), out_shape=(jax.Sh...  25.4 us
    unnamed x2, local copies, waits for them, and re-layouts  2.6 us

profile of v1, /device:TPU:0, one launch (start us, length us, event | category | flops | bytes accessed | tf_op | source)
XLA Modules:
  0.0 28.7 jit_solution(4975703998640507001)
XLA Ops:
  0.6 25.4 %shard_map.50 = (bf16[128,128]{1,0:T(8,128)(2,1)}, f32[2,128]{1,0:T(2,128)}) custom-call(s32[1,128]{1,0:T(1,128)} %pos_ref.1, s32[2]{0:T(128)} %cnt_ref.1, bf16[1,8192,128]{2,1,0:T(8,128)(2,1)} %coh_hbm.1), custom_call_target="tpu_custom_call" | custom-call | tf_op jit(solution)/shard_map/pallas_call | solution.py:257
  26.1 1.4 %copy.7 = bf16[128,128]{1,0:T(8,128)(2,1)} copy(bf16[128,128]{1,0:T(8,128)(2,1)} %get-tuple-element.4) | data formatting | bytes 65536
  27.4 1.2 %copy.8 = f32[2,128]{1,0:T(2,128)} copy(f32[2,128]{1,0:T(2,128)} %get-tuple-element.5) | data formatting | bytes 2048

commit v2 on v1

--- a/solution.py
+++ b/solution.py
@@ -9,16 +9,30 @@
 
 MESH = pl.DeviceIdType.MESH
 PIECES = 4
+PARTS = 2
+CHUNKS = 4
+
+
+def flip(index, mask):
+    out = index
+    w = 1
+    while w <= mask:
+        if mask & w:
+            out = out + w - 2 * w * lax.rem(index // w, 2)
+        w *= 2
+    return out
 
 
 def kernel(
     n_lat,
     n_seg,
-    pos_ref,
-    cnt_ref,
+    pos_hbm,
+    cnt_hbm,
     coh_hbm,
     semi_ref,
     excess_ref,
+    pos_ref,
+    cnt_ref,
     coh,
     gath,
     rows_out,
@@ -38,6 +52,7 @@
     cr_sem,
     xs_sem,
     xr_sem,
+    in_sem,
 ):
     lat = lax.axis_index("lat")
     seg = lax.axis_index("seg")
@@ -50,30 +65,34 @@
     steps = n_seg.bit_length() - 1
     f32, bf16, i32 = jnp.float32, jnp.bfloat16, jnp.int32
 
+    barrier = pltpu.get_barrier_semaphore()
+    lat_peers = [flip(lat, j) for j in range(n_lat)]
+    seg_peers = [flip(seg, 1 << b) for b in range(steps)]
+    far_first = list(range(n_lat - 1, 0, -1))
+    for j in far_first:
+        pl.semaphore_signal(barrier, inc=1, device_id=(seg, lat_peers[j]), device_id_type=MESH)
+    for b in range(steps):
+        pl.semaphore_signal(barrier, inc=1, device_id=(seg_peers[b], lat), device_id_type=MESH)
+
+    small = [
+        pltpu.make_async_copy(pos_hbm, pos_ref, in_sem.at[0]),
+        pltpu.make_async_copy(cnt_hbm, cnt_ref, in_sem.at[1]),
+    ]
+    for copy in small:
+        copy.start()
     piece = slice_bins // PIECES
     loads = []
     for k in range(PIECES):
         rng = pl.ds(k * piece, piece)
         loads.append(pltpu.make_async_copy(coh_hbm.at[0, rng], coh.at[rng], coh_sem.at[k]))
         loads[-1].start()
-
-    barrier = pltpu.get_barrier_semaphore()
-    lat_peers = [lax.rem(lat + j, n_lat) for j in range(n_lat)]
-    lat_back = [lax.rem(lat + n_lat - j, n_lat) for j in range(n_lat)]
-    seg_peers = []
-    for b in range(steps):
-        w = 1 << b
-        bit = lax.rem(seg // w, 2)
-        seg_peers.append(seg + w - 2 * w * bit)
-    for j in range(1, n_lat):
-        pl.semaphore_signal(barrier, inc=1, device_id=(seg, lat_peers[j]), device_id_type=MESH)
-    for b in range(steps):
-        pl.semaphore_signal(barrier, inc=1, device_id=(seg_peers[b], lat), device_id_type=MESH)
+    for copy in small:
+        copy.wait()
 
     pos = pos_ref[...]
     lane = lax.broadcasted_iota(i32, (1, points), 1)
     dest = (pos // 256) // slice_bins
-    rel = lax.rem(dest - lat + n_lat, n_lat)
+    rel = jnp.bitwise_xor(dest, jnp.full((1, points), lat, i32))
     hits = lax.broadcasted_iota(i32, (n_lat, points), 0) == rel
     hits_f = hits.astype(f32)
     tri = (
@@ -94,7 +113,7 @@
 
     pl.semaphore_wait(barrier, n_lat - 1 + steps)
     sends = []
-    for j in range(1, n_lat):
+    for j in far_first:
         copy = pltpu.make_async_remote_copy(
             src_ref=gath.at[0],
             dst_ref=gath.at[j],
@@ -142,43 +161,52 @@
     where_id = where_id.astype(f32).astype(bf16)
     zero = jnp.zeros_like(local)
 
-    held = jnp.zeros((total_slots, width), f32)
     per_piece = piece // depth
-    for k in range(PIECES):
-        loads[k].wait()
-        weights = jnp.concatenate(
-            [
-                jnp.where(where_id == jnp.asarray(k * per_piece + c, bf16), local, zero)
-                for c in range(per_piece)
-            ],
-            axis=1,
-        )
-        held = held + jnp.dot(
-            weights, coh[k * piece : (k + 1) * piece, :], preferred_element_type=f32
-        )
-
-    col = jnp.sum(jnp.where(live, held, 0.0), axis=0, keepdims=True)
-    for j in range(n_lat):
-        rows_out[j] = held[j * slots : (j + 1) * slots, :]
+    back = []
+    col = jnp.zeros((1, width), f32)
+    group = n_lat // PARTS
+    for part_id in range(PARTS - 1, -1, -1):
+        lo, hi = part_id * group * slots, (part_id + 1) * group * slots
+        held = jnp.zeros((hi - lo, width), f32)
+        for k in range(PIECES):
+            if part_id == PARTS - 1:
+                loads[k].wait()
+            weights = jnp.concatenate(
+                [
+                    jnp.where(
+                        where_id[lo:hi] == jnp.asarray(k * per_piece + c, bf16),
+                        local[lo:hi],
+                        zero[lo:hi],
+                    )
+                    for c in range(per_piece)
+                ],
+                axis=1,
+            )
+            held = held + jnp.dot(
+                weights, coh[k * piece : (k + 1) * piece, :], preferred_element_type=f32
+            )
+        for j in range((part_id + 1) * group - 1, part_id * group - 1, -1):
+            rows_out[j] = held[j * slots - lo : (j + 1) * slots - lo, :]
+        for j in range((part_id + 1) * group - 1, max(part_id * group, 1) - 1, -1):
+            copy = pltpu.make_async_remote_copy(
+                src_ref=rows_out.at[j],
+                dst_ref=rows_in.at[j],
+                send_sem=rs_sem.at[j],
+                recv_sem=rr_sem.at[j],
+                device_id=(seg, lat_peers[j]),
+                device_id_type=MESH,
+            )
+            copy.start()
+            back.append(copy)
+        col = col + jnp.sum(jnp.where(live[lo:hi], held, 0.0), axis=0, keepdims=True)
     col_out[...] = col
-    back = []
-    for j in range(1, n_lat):
-        copy = pltpu.make_async_remote_copy(
-            src_ref=rows_out.at[j],
-            dst_ref=rows_in.at[j],
-            send_sem=rs_sem.at[j],
-            recv_sem=rr_sem.at[j],
-            device_id=(seg, lat_back[j]),
-            device_id_type=MESH,
-        )
-        copy.start()
-        back.append(copy)
+    for j in far_first:
         copy = pltpu.make_async_remote_copy(
             src_ref=col_out,
             dst_ref=col_in.at[j],
             send_sem=cs_sem.at[j],
             recv_sem=cr_sem.at[j],
-            device_id=(seg, lat_back[j]),
+            device_id=(seg, lat_peers[j]),
             device_id_type=MESH,
         )
         copy.start()
@@ -196,43 +224,36 @@
     for j in range(1, n_lat):
         col = col + col_in[j]
 
-    half = points // 2
-    halves = [total[:half], total[half:]]
+    rows = points // CHUNKS
+    state = [total[c * rows : (c + 1) * rows] for c in range(CHUNKS)] + [col]
+    turn = [c // 2 + (c % 2) * (CHUNKS // 2) for c in range(CHUNKS)] + [CHUNKS]
     outs = []
-    for t in range(steps):
-        moves = []
-        order = (t, steps - 1 - t)
-        for h in range(2):
-            part[t, h] = halves[h]
-        psum[t] = col
-        for h in range(2):
+    arriving = {}
+    for t in range(steps + 1):
+        for c in turn:
+            box, box_in = (part, part_in) if c < CHUNKS else (psum, psum_in)
+            at = (c,) if c < CHUNKS else ()
+            if t > 0:
+                arriving[c].wait_recv()
+                state[c] = state[c] + box_in[(t - 1,) + at]
+            if t == steps:
+                continue
+            box[(t,) + at] = state[c]
+            bit = steps - 1 - t if CHUNKS // 2 <= c < CHUNKS else t
             copy = pltpu.make_async_remote_copy(
-                src_ref=part.at[t, h],
-                dst_ref=part_in.at[t, h],
-                send_sem=xs_sem.at[t, h],
-                recv_sem=xr_sem.at[t, h],
-                device_id=(seg_peers[order[h]], lat),
+                src_ref=box.at[(t,) + at],
+                dst_ref=box_in.at[(t,) + at],
+                send_sem=xs_sem.at[t, c],
+                recv_sem=xr_sem.at[t, c],
+                device_id=(seg_peers[bit], lat),
                 device_id_type=MESH,
             )
             copy.start()
-            moves.append(copy)
-        copy = pltpu.make_async_remote_copy(
-            src_ref=psum.at[t],
-            dst_ref=psum_in.at[t],
-            send_sem=xs_sem.at[t, 2],
-            recv_sem=xr_sem.at[t, 2],
-            device_id=(seg_peers[order[0]], lat),
-            device_id_type=MESH,
-        )
-        copy.start()
-        moves.append(copy)
-        for copy in moves:
-            copy.wait_recv()
-        halves = [halves[h] + part_in[t, h] for h in range(2)]
-        col = col + psum_in[t]
-        outs += moves
-
-    stat = jnp.concatenate(halves, axis=0) / n_seg
+            arriving[c] = copy
+            outs.append(copy)
+    col = state[CHUNKS]
+
+    stat = jnp.concatenate(state[:CHUNKS], axis=0) / n_seg
     semi_ref[...] = stat.astype(semi_ref.dtype)
     global_mean = (col / n_seg) / total_count
     row = lax.broadcasted_iota(i32, (block_size, width), 0)
@@ -246,6 +267,17 @@
         copy.wait_send()
 
 
+def deliver(semi_ref, excess_ref, semi_out, excess_out, sem):
+    copies = [
+        pltpu.make_async_copy(semi_ref, semi_out, sem.at[0]),
+        pltpu.make_async_copy(excess_ref, excess_out, sem.at[1]),
+    ]
+    for copy in copies:
+        copy.start()
+    for copy in copies:
+        copy.wait()
+
+
 def shards(n_lat, n_seg, coh_map, positions, counts):
     _, slice_bins, width = coh_map.shape
     points = positions.shape[1]
@@ -254,15 +286,15 @@
     steps = n_seg.bit_length() - 1
     f32 = jnp.float32
     dma = pltpu.SemaphoreType.DMA
-    return pl.pallas_call(
+    made = pl.pallas_call(
         functools.partial(kernel, n_lat, n_seg),
         out_shape=(
-            jax.ShapeDtypeStruct((points, width), jnp.bfloat16),
-            jax.ShapeDtypeStruct((blocks, width), f32),
+            pltpu.VMEM((points, width), jnp.bfloat16),
+            pltpu.VMEM((blocks, width), f32),
         ),
         in_specs=[
-            pl.BlockSpec(memory_space=pltpu.VMEM),
-            pl.BlockSpec(memory_space=pltpu.SMEM),
+            pl.BlockSpec(memory_space=pl.ANY),
+            pl.BlockSpec(memory_space=pl.ANY),
             pl.BlockSpec(memory_space=pl.ANY),
         ],
         out_specs=(
@@ -270,14 +302,16 @@
             pl.BlockSpec(memory_space=pltpu.VMEM),
         ),
         scratch_shapes=[
+            pltpu.VMEM((1, points), jnp.int32),
+            pltpu.SMEM((blocks,), jnp.int32),
             pltpu.VMEM((slice_bins, width), coh_map.dtype),
             pltpu.VMEM((n_lat, 4, points), jnp.int32),
             pltpu.VMEM((n_lat, slots, width), f32),
             pltpu.VMEM((n_lat, slots, width), f32),
             pltpu.VMEM((1, width), f32),
             pltpu.VMEM((n_lat, 1, width), f32),
-            pltpu.VMEM((steps, 2, points // 2, width), f32),
-            pltpu.VMEM((steps, 2, points // 2, width), f32),
+            pltpu.VMEM((steps, CHUNKS, points // CHUNKS, width), f32),
+            pltpu.VMEM((steps, CHUNKS, points // CHUNKS, width), f32),
             pltpu.VMEM((steps, 1, width), f32),
             pltpu.VMEM((steps, 1, width), f32),
             dma((PIECES,)),
@@ -287,11 +321,20 @@
             dma((n_lat,)),
             dma((n_lat,)),
             dma((n_lat,)),
-            dma((steps, 3)),
-            dma((steps, 3)),
+            dma((steps, CHUNKS + 1)),
+            dma((steps, CHUNKS + 1)),
+            dma((2,)),
         ],
         compiler_params=pltpu.CompilerParams(collective_id=0, has_side_effects=True),
     )(positions, counts, coh_map)
+    made = [pltpu.with_memory_space_constraint(x, pltpu.VMEM) for x in made]
+    return pl.pallas_call(
+        deliver,
+        out_shape=tuple(jax.ShapeDtypeStruct(x.shape, x.dtype) for x in made),
+        in_specs=[pl.BlockSpec(memory_space=pltpu.VMEM)] * 2,
+        out_specs=(pl.BlockSpec(memory_space=pl.ANY),) * 2,
+        scratch_shapes=[dma((2,))],
+    )(*made)
 
 
 def solution(mesh):

time: 28.9 us -> 24.2 us (0.84)
  local copies, waits for them, and re-layouts: 2.6 us -> 0 us
  Pallas kernels: 25.4 us -> 23.4 us
    unnamed x2 -> x0, local copies, waits for them, and re-layouts: 2.6 us -> none
    pallas_call x1 -> x2, Pallas kernels: 25.4 us -> 23.4 us  [the longest x1 22.8 us: shards(): pl.pallas_call(functools.partial(kernel, n_lat, n_seg), out_shape=(pltpu....]
where the time goes in v2:
time: 24.2 us; the launch traced here: 24.1 us
  Pallas kernels  23.4 us (97%)
  between operations  0.64 us (3%)
    pallas_call x1, Pallas kernels, shards(): pl.pallas_call(functools.partial(kernel, n_lat, n_seg), out_shape=(pltpu....  22.8 us
    pallas_call x1, Pallas kernels, shards(): pl.pallas_call(deliver, out_shape=tuple((jax.ShapeDtypeStruct(x.shape, x....  0.64 us

profile of v2, /device:TPU:0, one launch (start us, length us, event | category | flops | bytes accessed | tf_op | source)
XLA Modules:
  0.0 24.1 jit_solution(661697519816049790)
XLA Ops:
  0.6 22.8 %shard_map.50 = (bf16[128,128]{1,0:T(8,128)(2,1)S(1)}, f32[2,128]{1,0:T(2,128)S(1)}) custom-call(s32[1,128]{1,0:T(1,128)} %pos_hbm.1, s32[2]{0:T(128)} %cnt_hbm.1, bf16[1,8192,128]{2,1,0:T(8,128)(2,1)} %coh_hbm.1), custom_call_target="tpu_custom_call" | custom-call | tf_op jit(solution)/shard_map/pallas_call | solution.py:289
  23.4 0.6 %shard_map.51 = (bf16[128,128]{1,0:T(8,128)(2,1)}, f32[2,128]{1,0:T(2,128)}) custom-call(bf16[128,128]{1,0:T(8,128)(2,1)S(1)} %get-tuple-element.4.semi_ref, f32[2,128]{1,0:T(2,128)S(1)} %get-tuple-element.5.excess_ref), custom_call_target="tpu_custom_call" | custom-call | tf_op jit(solution)/shard_map/pallas_call | solution.py:331

commit v3 on v2

--- a/solution.py
+++ b/solution.py
@@ -9,8 +9,7 @@
 
 MESH = pl.DeviceIdType.MESH
 PIECES = 4
-PARTS = 2
-CHUNKS = 4
+PARTS = 4
 
 
 def flip(index, mask):
@@ -62,17 +61,15 @@
     block_size = points // blocks
     slots = 2 * points // n_lat
     total_slots = n_lat * slots
-    steps = n_seg.bit_length() - 1
     f32, bf16, i32 = jnp.float32, jnp.bfloat16, jnp.int32
 
     barrier = pltpu.get_barrier_semaphore()
     lat_peers = [flip(lat, j) for j in range(n_lat)]
-    seg_peers = [flip(seg, 1 << b) for b in range(steps)]
     far_first = list(range(n_lat - 1, 0, -1))
     for j in far_first:
         pl.semaphore_signal(barrier, inc=1, device_id=(seg, lat_peers[j]), device_id_type=MESH)
-    for b in range(steps):
-        pl.semaphore_signal(barrier, inc=1, device_id=(seg_peers[b], lat), device_id_type=MESH)
+    for b in range(1, n_seg):
+        pl.semaphore_signal(barrier, inc=1, device_id=(flip(seg, b), lat), device_id_type=MESH)
 
     small = [
         pltpu.make_async_copy(pos_hbm, pos_ref, in_sem.at[0]),
@@ -111,7 +108,7 @@
     gath[0, 2:3, :] = valid
     gath[0, 3:4, :] = valid
 
-    pl.semaphore_wait(barrier, n_lat - 1 + steps)
+    pl.semaphore_wait(barrier, n_lat - 1 + n_seg - 1)
     sends = []
     for j in far_first:
         copy = pltpu.make_async_remote_copy(
@@ -128,56 +125,51 @@
     pick_t = (lax.broadcasted_iota(i32, (total_slots, points), 0) == sid).astype(f32)
     pick = pick_t.T.astype(bf16)
 
-    for copy in sends:
-        copy.wait_recv()
-
-    base = lat * (slice_bins * 256)
-    flag = slice_bins * 256
+    arriving = {j: copy for j, copy in zip(far_first, sends)}
+
+    pos_bits = 8
+    bin_bits = (slice_bins - 1).bit_length()
+    depth = min(256, slice_bins)
+    depth_bits = depth.bit_length() - 1
+    base = lat * (slice_bins << pos_bits)
+    flag = slice_bins << pos_bits
     sub = lax.broadcasted_iota(i32, (slots, points), 0)
-    cols = []
+    group = n_lat // PARTS
+    span = group * slots
+    bins = lax.broadcasted_iota(i32, (span, depth), 1)
+    zero = jnp.zeros((span, depth), bf16)
+    per_piece = piece // depth
     count = jnp.zeros((1, points), i32)
-    for j in range(n_lat):
-        code = (gath[j, 1:2, :] - base + flag * (1 + gath[j, 2:3, :])).astype(f32)
-        here = (gath[j, 0:1, :] - j * slots) == sub
-        cols.append(jnp.sum(jnp.where(here, code, 0.0), axis=1, keepdims=True))
-        count = count + gath[j, 2:3, :]
-    code = jnp.concatenate(cols, axis=0).astype(i32)
-    total_count = jnp.sum(count.astype(f32), axis=1, keepdims=True)
-    present = code >= flag
-    live = code >= 2 * flag
-    off = code % flag
-    low = off // 256
-    upper = (off % 256).astype(f32) / 256.0
-    depth = min(256, slice_bins)
-    chunk = low // depth
-    in_chunk = low % depth
-    bins = lax.broadcasted_iota(i32, (total_slots, depth), 1)
-    local = jnp.where(bins == in_chunk, 1.0 - upper, 0.0) + jnp.where(
-        bins == (in_chunk + 1) % depth, upper, 0.0
-    )
-    where_id = jnp.where(bins < in_chunk, chunk + 1, chunk)
-    where_id = jnp.where(present, where_id, -1)
-    local = local.astype(bf16)
-    where_id = where_id.astype(f32).astype(bf16)
-    zero = jnp.zeros_like(local)
-
-    per_piece = piece // depth
-    back = []
     col = jnp.zeros((1, width), f32)
-    group = n_lat // PARTS
-    for part_id in range(PARTS - 1, -1, -1):
-        lo, hi = part_id * group * slots, (part_id + 1) * group * slots
-        held = jnp.zeros((hi - lo, width), f32)
+    back, col_back = [], []
+    coming = {}
+    for part_id in range(PARTS):
+        owners = list(range(part_id * group, (part_id + 1) * group))
+        cols = []
+        for j in owners:
+            if j > 0:
+                arriving[j].wait_recv()
+            live_row = gath[j, 2:3, :]
+            code = (gath[j, 1:2, :] - base + flag * (1 + live_row)).astype(f32)
+            here = (gath[j, 0:1, :] - j * slots) == sub
+            cols.append(jnp.sum(jnp.where(here, code, 0.0), axis=1, keepdims=True))
+            count = count + live_row
+        code = jnp.concatenate(cols, axis=0).astype(i32)
+        kind = lax.shift_right_logical(code, bin_bits + pos_bits)
+        low = lax.shift_right_logical(code & (flag - 1), pos_bits)
+        upper = (code & ((1 << pos_bits) - 1)).astype(f32) * (1.0 / (1 << pos_bits))
+        chunk = jnp.where(kind > 0, lax.shift_right_logical(low, depth_bits), -2)
+        in_chunk = low & (depth - 1)
+        local = jnp.where(bins == in_chunk, 1.0 - upper, 0.0)
+        local = jnp.where(bins == ((in_chunk + 1) & (depth - 1)), upper, local).astype(bf16)
+        where_id = jnp.where(bins < in_chunk, chunk + 1, chunk).astype(f32).astype(bf16)
+        held = jnp.zeros((span, width), f32)
         for k in range(PIECES):
-            if part_id == PARTS - 1:
+            if part_id == 0:
                 loads[k].wait()
             weights = jnp.concatenate(
                 [
-                    jnp.where(
-                        where_id[lo:hi] == jnp.asarray(k * per_piece + c, bf16),
-                        local[lo:hi],
-                        zero[lo:hi],
-                    )
+                    jnp.where(where_id == jnp.asarray(k * per_piece + c, bf16), local, zero)
                     for c in range(per_piece)
                 ],
                 axis=1,
@@ -185,9 +177,11 @@
             held = held + jnp.dot(
                 weights, coh[k * piece : (k + 1) * piece, :], preferred_element_type=f32
             )
-        for j in range((part_id + 1) * group - 1, part_id * group - 1, -1):
-            rows_out[j] = held[j * slots - lo : (j + 1) * slots - lo, :]
-        for j in range((part_id + 1) * group - 1, max(part_id * group, 1) - 1, -1):
+        for i, j in enumerate(owners):
+            rows_out[j] = held[i * slots : (i + 1) * slots, :]
+        for j in reversed(owners):
+            if j == 0:
+                continue
             copy = pltpu.make_async_remote_copy(
                 src_ref=rows_out.at[j],
                 dst_ref=rows_in.at[j],
@@ -198,7 +192,8 @@
             )
             copy.start()
             back.append(copy)
-        col = col + jnp.sum(jnp.where(live[lo:hi], held, 0.0), axis=0, keepdims=True)
+            coming[j] = copy
+        col = col + jnp.sum(jnp.where(kind > 1, held, 0.0), axis=0, keepdims=True)
     col_out[...] = col
     for j in far_first:
         copy = pltpu.make_async_remote_copy(
@@ -210,50 +205,61 @@
             device_id_type=MESH,
         )
         copy.start()
-        back.append(copy)
-    for copy in back:
-        copy.wait_recv()
-
-    own = [rows_out[0]] + [rows_in[j] for j in range(1, n_lat)]
-    got = jnp.concatenate(own, axis=0)
-    high = got.astype(bf16)
-    rest = (got - high.astype(f32)).astype(bf16)
-    total = jnp.dot(pick, high, preferred_element_type=f32) + jnp.dot(
-        pick, rest, preferred_element_type=f32
-    )
-    for j in range(1, n_lat):
-        col = col + col_in[j]
-
-    rows = points // CHUNKS
-    state = [total[c * rows : (c + 1) * rows] for c in range(CHUNKS)] + [col]
-    turn = [c // 2 + (c % 2) * (CHUNKS // 2) for c in range(CHUNKS)] + [CHUNKS]
+        col_back.append(copy)
+    total_count = jnp.sum(count.astype(f32), axis=1, keepdims=True)
+
+    total = jnp.zeros((points, width), f32)
+    for part_id in range(PARTS):
+        owners = list(range(part_id * group, (part_id + 1) * group))
+        got = []
+        for j in owners:
+            if j > 0:
+                coming[j].wait_recv()
+            got.append(rows_in[j] if j > 0 else rows_out[0])
+        got = jnp.concatenate(got, axis=0)
+        high = got.astype(bf16)
+        rest = (got - high.astype(f32)).astype(bf16)
+        mine = pick[:, part_id * span : (part_id + 1) * span]
+        total = total + jnp.dot(
+            jnp.concatenate([mine, mine], axis=1),
+            jnp.concatenate([high, rest], axis=0),
+            preferred_element_type=f32,
+        )
+
+    part[0] = total
     outs = []
-    arriving = {}
-    for t in range(steps + 1):
-        for c in turn:
-            box, box_in = (part, part_in) if c < CHUNKS else (psum, psum_in)
-            at = (c,) if c < CHUNKS else ()
-            if t > 0:
-                arriving[c].wait_recv()
-                state[c] = state[c] + box_in[(t - 1,) + at]
-            if t == steps:
-                continue
-            box[(t,) + at] = state[c]
-            bit = steps - 1 - t if CHUNKS // 2 <= c < CHUNKS else t
+
+    def tell(box, box_in, q):
+        for m in range(n_seg - 1, 0, -1):
             copy = pltpu.make_async_remote_copy(
-                src_ref=box.at[(t,) + at],
-                dst_ref=box_in.at[(t,) + at],
-                send_sem=xs_sem.at[t, c],
-                recv_sem=xr_sem.at[t, c],
-                device_id=(seg_peers[bit], lat),
+                src_ref=box.at[0],
+                dst_ref=box_in.at[m],
+                send_sem=xs_sem.at[m, q],
+                recv_sem=xr_sem.at[m, q],
+                device_id=(flip(seg, m), lat),
                 device_id_type=MESH,
             )
             copy.start()
-            arriving[c] = copy
             outs.append(copy)
-    col = state[CHUNKS]
-
-    stat = jnp.concatenate(state[:CHUNKS], axis=0) / n_seg
+
+    def tree(terms):
+        w = 1
+        while w < n_seg:
+            terms = [terms[i] + terms[i + 1] for i in range(0, len(terms), 2)]
+            w *= 2
+        return terms[0]
+
+    tell(part, part_in, 0)
+    for copy in col_back:
+        copy.wait_recv()
+    for j in range(1, n_lat):
+        col = col + col_in[j]
+    psum[0] = col
+    tell(psum, psum_in, 1)
+    for copy in outs:
+        copy.wait_recv()
+    stat = tree([total] + [part_in[m] for m in range(1, n_seg)]) / n_seg
+    col = tree([col] + [psum_in[m] for m in range(1, n_seg)])
     semi_ref[...] = stat.astype(semi_ref.dtype)
     global_mean = (col / n_seg) / total_count
     row = lax.broadcasted_iota(i32, (block_size, width), 0)
@@ -263,7 +269,7 @@
         mean = block_sum / jnp.full((1, width), cnt_ref[b], i32).astype(f32)
         excess_ref[b : b + 1, :] = mean - global_mean
 
-    for copy in sends + back + outs:
+    for copy in sends + back + col_back + outs:
         copy.wait_send()
 
 
@@ -283,7 +289,6 @@
     points = positions.shape[1]
     blocks = counts.shape[0]
     slots = 2 * points // n_lat
-    steps = n_seg.bit_length() - 1
     f32 = jnp.float32
     dma = pltpu.SemaphoreType.DMA
     made = pl.pallas_call(
@@ -310,10 +315,10 @@
             pltpu.VMEM((n_lat, slots, width), f32),
             pltpu.VMEM((1, width), f32),
             pltpu.VMEM((n_lat, 1, width), f32),
-            pltpu.VMEM((steps, CHUNKS, points // CHUNKS, width), f32),
-            pltpu.VMEM((steps, CHUNKS, points // CHUNKS, width), f32),
-            pltpu.VMEM((steps, 1, width), f32),
-            pltpu.VMEM((steps, 1, width), f32),
+            pltpu.VMEM((n_seg, points, width), f32),
+            pltpu.VMEM((n_seg, points, width), f32),
+            pltpu.VMEM((n_seg, 1, width), f32),
+            pltpu.VMEM((n_seg, 1, width), f32),
             dma((PIECES,)),
             dma((n_lat,)),
             dma((n_lat,)),
@@ -321,8 +326,8 @@
             dma((n_lat,)),
             dma((n_lat,)),
             dma((n_lat,)),
-            dma((steps, CHUNKS + 1)),
-            dma((steps, CHUNKS + 1)),
+            dma((n_seg, 2)),
+            dma((n_seg, 2)),
             dma((2,)),
         ],
         compiler_params=pltpu.CompilerParams(collective_id=0, has_side_effects=True),

time: 24.2 us -> 21.8 us (0.901)
  Pallas kernels: 23.4 us -> 21 us
    pallas_call x1, Pallas kernels: 22.8 us -> 20.4 us  [shards(): pl.pallas_call(functools.partial(kernel, n_lat, n_seg), out_shape=(pltpu....]
where the time goes in v3:
time: 21.8 us; the launch traced here: 21.6 us
  Pallas kernels  21 us (96%)
  between operations  0.64 us (3%)
    pallas_call x1, Pallas kernels, shards(): pl.pallas_call(functools.partial(kernel, n_lat, n_seg), out_shape=(pltpu....  20.4 us
    pallas_call x1, Pallas kernels, shards(): pl.pallas_call(deliver, out_shape=tuple((jax.ShapeDtypeStruct(x.shape, x....  0.64 us

profile of v3, /device:TPU:0, one launch (start us, length us, event | category | flops | bytes accessed | tf_op | source)
XLA Modules:
  0.0 21.6 jit_solution(15767189330493626978)
XLA Ops:
  0.6 20.4 %shard_map.50 = (bf16[128,128]{1,0:T(8,128)(2,1)S(1)}, f32[2,128]{1,0:T(2,128)S(1)}) custom-call(s32[1,128]{1,0:T(1,128)} %pos_hbm.1, s32[2]{0:T(128)} %cnt_hbm.1, bf16[1,8192,128]{2,1,0:T(8,128)(2,1)} %coh_hbm.1), custom_call_target="tpu_custom_call" | custom-call | tf_op jit(solution)/shard_map/pallas_call | solution.py:294
  21.0 0.6 %shard_map.51 = (bf16[128,128]{1,0:T(8,128)(2,1)}, f32[2,128]{1,0:T(2,128)}) custom-call(bf16[128,128]{1,0:T(8,128)(2,1)S(1)} %get-tuple-element.4.semi_ref, f32[2,128]{1,0:T(2,128)S(1)} %get-tuple-element.5.excess_ref), custom_call_target="tpu_custom_call" | custom-call | tf_op jit(solution)/shard_map/pallas_call | solution.py:336

commit v4 on v3

--- a/solution.py
+++ b/solution.py
@@ -8,8 +8,9 @@
 from jax.sharding import PartitionSpec as P
 
 MESH = pl.DeviceIdType.MESH
-PIECES = 4
+PIECES = 1
 PARTS = 4
+CUTS = 2
 
 
 def flip(index, mask):
@@ -208,7 +209,8 @@
         col_back.append(copy)
     total_count = jnp.sum(count.astype(f32), axis=1, keepdims=True)
 
-    total = jnp.zeros((points, width), f32)
+    highs = []
+    rests = []
     for part_id in range(PARTS):
         owners = list(range(part_id * group, (part_id + 1) * group))
         got = []
@@ -218,22 +220,16 @@
             got.append(rows_in[j] if j > 0 else rows_out[0])
         got = jnp.concatenate(got, axis=0)
         high = got.astype(bf16)
-        rest = (got - high.astype(f32)).astype(bf16)
-        mine = pick[:, part_id * span : (part_id + 1) * span]
-        total = total + jnp.dot(
-            jnp.concatenate([mine, mine], axis=1),
-            jnp.concatenate([high, rest], axis=0),
-            preferred_element_type=f32,
-        )
-
-    part[0] = total
+        highs.append(high)
+        rests.append((got - high.astype(f32)).astype(bf16))
+    spread = jnp.concatenate(highs + rests, axis=0)
     outs = []
 
-    def tell(box, box_in, q):
+    def tell(src, dsts, q):
         for m in range(n_seg - 1, 0, -1):
             copy = pltpu.make_async_remote_copy(
-                src_ref=box.at[0],
-                dst_ref=box_in.at[m],
+                src_ref=src,
+                dst_ref=dsts[m],
                 send_sem=xs_sem.at[m, q],
                 recv_sem=xr_sem.at[m, q],
                 device_id=(flip(seg, m), lat),
@@ -242,6 +238,15 @@
             copy.start()
             outs.append(copy)
 
+    part_rows = points // CUTS
+    for h in range(CUTS):
+        rng = pl.ds(h * part_rows, part_rows)
+        mine = pick[h * part_rows : (h + 1) * part_rows]
+        part[0, rng] = jnp.dot(
+            jnp.concatenate([mine, mine], axis=1), spread, preferred_element_type=f32
+        )
+        tell(part.at[0, rng], [part_in.at[m, rng] for m in range(n_seg)], h)
+
     def tree(terms):
         w = 1
         while w < n_seg:
@@ -249,16 +254,15 @@
             w *= 2
         return terms[0]
 
-    tell(part, part_in, 0)
     for copy in col_back:
         copy.wait_recv()
     for j in range(1, n_lat):
         col = col + col_in[j]
     psum[0] = col
-    tell(psum, psum_in, 1)
+    tell(psum.at[0], [psum_in.at[m] for m in range(n_seg)], CUTS)
     for copy in outs:
         copy.wait_recv()
-    stat = tree([total] + [part_in[m] for m in range(1, n_seg)]) / n_seg
+    stat = tree([part[0]] + [part_in[m] for m in range(1, n_seg)]) / n_seg
     col = tree([col] + [psum_in[m] for m in range(1, n_seg)])
     semi_ref[...] = stat.astype(semi_ref.dtype)
     global_mean = (col / n_seg) / total_count
@@ -326,8 +330,8 @@
             dma((n_lat,)),
             dma((n_lat,)),
             dma((n_lat,)),
-            dma((n_seg, 2)),
-            dma((n_seg, 2)),
+            dma((n_seg, CUTS + 1)),
+            dma((n_seg, CUTS + 1)),
             dma((2,)),
         ],
         compiler_params=pltpu.CompilerParams(collective_id=0, has_side_effects=True),

time: 21.8 us -> 21.7 us (level)
  no operation moved by 1% of the time
where the time goes in v4:
time: 21.7 us; the launch traced here: 21.5 us
  Pallas kernels  20.9 us (96%)
  between operations  0.64 us (3%)
    pallas_call x1, Pallas kernels, shards(): pl.pallas_call(functools.partial(kernel, n_lat, n_seg), out_shape=(pltpu....  20.3 us
    pallas_call x1, Pallas kernels, shards(): pl.pallas_call(deliver, out_shape=tuple((jax.ShapeDtypeStruct(x.shape, x....  0.64 us

profile of v4, /device:TPU:0, one launch (start us, length us, event | category | flops | bytes accessed | tf_op | source)
XLA Modules:
  0.0 21.5 jit_solution(8880055709680919373)
XLA Ops:
  0.6 20.3 %shard_map.50 = (bf16[128,128]{1,0:T(8,128)(2,1)S(1)}, f32[2,128]{1,0:T(2,128)S(1)}) custom-call(s32[1,128]{1,0:T(1,128)} %pos_hbm.1, s32[2]{0:T(128)} %cnt_hbm.1, bf16[1,8192,128]{2,1,0:T(8,128)(2,1)} %coh_hbm.1), custom_call_target="tpu_custom_call" | custom-call | tf_op jit(solution)/shard_map/pallas_call | solution.py:298
  20.9 0.6 %shard_map.51 = (bf16[128,128]{1,0:T(8,128)(2,1)}, f32[2,128]{1,0:T(2,128)}) custom-call(bf16[128,128]{1,0:T(8,128)(2,1)S(1)} %get-tuple-element.4.semi_ref, f32[2,128]{1,0:T(2,128)S(1)} %get-tuple-element.5.excess_ref), custom_call_target="tpu_custom_call" | custom-call | tf_op jit(solution)/shard_map/pallas_call | solution.py:340
